TPU v7x, 32 devices: a whole 2x2x4 slice. The times are simulated.
32 devices in a mesh: sp: 8 (over z, y), tp: 4 (over x, core).
Axes of the slice: x: 2, y: 2, z: 4, core: 2. Of those that a mesh axis runs over, the one named last changes fastest.
Arguments:
- decay_rate: float32 [1, 4096, 4096], P(None, 'sp', 'tp'), may hold values from 0.2 to 2
- drive_in: bfloat16 [1, 4096, 4096], P(None, 'sp', 'tp'), may hold values from -6 to 6
- gate_in: bfloat16 [1, 4096, 4096], P(None, 'sp', 'tp'), may hold values from -6 to 6
- norm_gain: float32 [4096], P('tp'), may hold values from 0.25 to 1.75
Outputs:
- filtered: bfloat16 [1, 4096, 4096], P(None, 'sp', 'tp')
All inputs are finite; a program needn't handle non-finite values.
Results may differ from a plain program's by a relative error of at most 0.001.
Values sent between devices are 32-bit elements; how exact they have to be, the bound alone decides.
No kernel may reach another device: no remote copies, remote signals or barrier semaphores. Data moves between devices by JAX's collectives and lax.ppermute only.
A program may use at most 64 MiB of HBM per device.

v0:
```python
import jax
import jax.numpy as jnp
from jax import lax
from jax.sharding import PartitionSpec as P


def prefix(value, axis, join, neutral, backward):
    count, mine = (lax.axis_size(axis), lax.axis_index(axis))
    pieces = jax.tree.map(lambda part: lax.all_gather(part, axis), value)
    if backward:
        pieces = jax.tree.map(lambda part: part[::-1], pieces)
        mine = count - 1 - mine
    total = jax.tree.map(
        lambda part, zero: jnp.full_like(part, 0) + jnp.asarray(zero, part.dtype), value, neutral
    )

    def hop(position, total):
        longer = join(total, jax.tree.map(lambda part: part[position], pieces))
        return jax.tree.map(lambda new, old: jnp.where(position < mine, new, old), longer, total)

    return lax.fori_loop(0, count - 1, hop, total)


def join_pair(earlier, later):
    return (earlier[0] * later[0], later[0] * earlier[1] + later[1])


def body(decay_rate, drive_in, gate_in, norm_gain):
    total_length = decay_rate.shape[1] * lax.axis_size("sp")
    keep = jnp.exp(-decay_rate / total_length)
    push = drive_in.astype(jnp.float32) * total_length ** (-0.5)
    product, forward = lax.associative_scan(join_pair, (keep, push), axis=1)
    entering_forward = prefix(
        (product[:, -1], forward[:, -1]),
        "sp",
        join_pair,
        (jnp.ones_like(keep[:, 0]), jnp.zeros_like(push[:, 0])),
        False,
    )
    forward = forward + product * entering_forward[1][:, None]
    product, backward = lax.associative_scan(join_pair, (keep, push), axis=1, reverse=True)
    entering_backward = prefix(
        (product[:, 0], backward[:, 0]),
        "sp",
        join_pair,
        (jnp.ones_like(keep[:, 0]), jnp.zeros_like(push[:, 0])),
        True,
    )
    backward = backward + product * entering_backward[1][:, None]
    states = forward + backward
    gated = states * jax.nn.sigmoid(gate_in.astype(jnp.float32))
    power = lax.psum(jnp.sum(gated * gated, axis=-1, keepdims=True), "tp") / (
        gated.shape[-1] * lax.axis_size("tp")
    )
    filtered = (gated * lax.rsqrt(power + 1e-06) * norm_gain).astype(jnp.bfloat16)
    return filtered


def solution(mesh):
    in_specs = (P(None, "sp", "tp"), P(None, "sp", "tp"), P(None, "sp", "tp"), P("tp"))
    out_specs = P(None, "sp", "tp")
    return jax.shard_map(body, mesh=mesh, in_specs=in_specs, out_specs=out_specs, check_vma=False)
```

profile of v0, /device:TPU:0, one launch (start us, length us, event | category | flops | bytes accessed | tf_op | source)
XLA Modules:
  0.0 348.7 jit_solution(10183357181414482121)
XLA Ops:
  0.0 1.9 multiply_exponential_fusion
  2.4 2.8 slice.542
  5.2 8.9 %slice.633 = f32[1,256,1024]{2,1,0:T(8,128)} reverse(f32[1,256,1024]{2,1,0:T(8,128)} %slice.542), dimensions={1} | reverse | bytes 2097152 | tf_op jit(solution)/shard_map/slice | solution.py:41
  14.1 5.2 %slice.629 = f32[1,256,1024]{2,1,0:T(8,128)} reverse(f32[1,256,1024]{2,1,0:T(8,128)S(1)} %slice.546), dimensions={1} | reverse | bytes 2097152 | tf_op jit(solution)/shard_map/slice | solution.py:41
  19.3 2.8 slice.627
  22.1 2.9 slice.541
  25.0 9.1 %slice.628 = f32[1,255,1024]{2,1,0:T(8,128)} reverse(f32[1,255,1024]{2,1,0:T(8,128)} %slice.627), dimensions={1} | reverse | bytes 2088960 | tf_op jit(solution)/shard_map/slice | solution.py:41
  34.1 1.5 broadcast_multiply_fusion.1
  35.6 3.0 slice.606
  38.6 2.8 slice.544
  41.4 2.9 slice.543
  44.3 2.3 multiply_add_fusion.1
  46.6 1.5 slice.604
  48.1 1.5 slice.550
  49.6 1.5 slice.549
  51.0 1.5 slice.552
  52.5 1.4 slice.548
  62.7 2.1 pad.235
  64.9 4.6 %pad.253 = f32[1,256,1024]{2,1,0:T(8,128)} pad(f32[1,128,1024]{2,1,0:T(8,128)} %add.464, f32[]{:T(128)} %constant.61.clone.1), padding=0_0_0x1_0_1x0_0_0 | pad | bytes 1572868 | tf_op jit(solution)/shard_map/pad | solution.py:32
  69.4 2.6 fusion.1
  75.8 8.8 %pad.236 = f32[1,512,1024]{2,1,0:T(8,128)} pad(f32[1,256,1024]{2,1,0:T(8,128)} %pad_maximum_fusion, f32[]{:T(128)} %constant.61.clone.1), padding=0_0_0x0_1_1x0_0_0 | pad | bytes 3145732 | tf_op jit(solution)/shard_map/pad | solution.py:32
  84.6 4.8 %pad.237 = f32[1,512,1024]{2,1,0:T(8,128)} pad(f32[1,256,1024]{2,1,0:T(8,128)S(1)} %copy-done.6, f32[]{:T(128)} %constant.61.clone.1), padding=0_0_0x1_0_1x0_0_0 | pad | bytes 3145732 | tf_op jit(solution)/shard_map/pad | solution.py:32
  90.3 32.4 %all_gather.13 = f32[8,1,1024]{2,1,0:T(1,128)S(1)} all-gather(f32[1,1,1024]{2,1,0:T(1,128)S(1)} %slice_add_fusion.4), channel_id=1, replica_groups=mesh['sp'=8,'tp'=4] {'sp'}, dimensions={0}, use_global_device_ids=true | all-gather | bytes 36864 | tf_op jit(solution)/shard_map/all_gather | solution.py:9
  122.8 8.6 %pad.255 = f32[1,512,1024]{2,1,0:T(8,128)} pad(f32[1,256,1024]{2,1,0:T(8,128)} %add.465, f32[]{:T(128)} %constant.61.clone.1), padding=0_0_0x1_0_1x0_0_0 | pad | bytes 3145732 | tf_op jit(solution)/shard_map/pad | solution.py:32
  132.1 30.8 %all_gather.12 = f32[8,1,1024]{2,1,0:T(1,128)S(1)} all-gather(f32[1,1,1024]{2,1,0:T(1,128)S(1)} %slice_add_fusion.5), channel_id=1, replica_groups=mesh['sp'=8,'tp'=4] {'sp'}, dimensions={0}, use_global_device_ids=true | all-gather | bytes 36864 | tf_op jit(solution)/shard_map/all_gather | solution.py:9
  163.2 10.7 %reverse.9 = f32[1,512,1024]{2,1,0:T(8,128)} reverse(bf16[1,512,1024]{2,1,0:T(8,128)(2,1)S(1)} %copy-done.4), dimensions={1} | reverse | bytes 3145728 | tf_op jit(solution)/shard_map/reverse
  173.9 1.8 broadcast_multiply_fusion
  175.7 3.0 slice.693
  178.6 2.8 slice.631
  181.4 2.8 slice.630
  184.3 2.3 fusion.23
  187.1 1.5 slice.634
  188.6 1.5 slice.691
  198.1 2.1 pad.289
  200.2 4.6 %pad.271 = f32[1,256,1024]{2,1,0:T(8,128)} pad(f32[1,128,1024]{2,1,0:T(8,128)} %add.489, f32[]{:T(128)} %constant.61.clone.1), padding=0_0_0x1_0_1x0_0_0 | pad | bytes 1572868 | tf_op jit(solution)/shard_map/pad | solution.py:41
  204.8 2.6 add_multiply_fusion
  211.2 8.7 %pad.290 = f32[1,512,1024]{2,1,0:T(8,128)} pad(f32[1,256,1024]{2,1,0:T(8,128)} %pad_maximum_fusion.3, f32[]{:T(128)} %constant.61.clone.1), padding=0_0_0x0_1_1x0_0_0 | pad | bytes 3145732 | tf_op jit(solution)/shard_map/pad | solution.py:41
  219.9 4.8 %pad.291 = f32[1,512,1024]{2,1,0:T(8,128)} pad(f32[1,256,1024]{2,1,0:T(8,128)S(1)} %copy-done.7, f32[]{:T(128)} %constant.61.clone.1), padding=0_0_0x1_0_1x0_0_0 | pad | bytes 3145732 | tf_op jit(solution)/shard_map/pad | solution.py:41
  225.5 4.2 %add.502 = f32[1,512,1024]{2,1,0:T(8,128)} add(f32[1,512,1024]{2,1,0:T(8,128)} %pad.290, f32[1,512,1024]{2,1,0:T(8,128)} %pad.291) | non-fusion elementwise | flops 524288 | bytes 6291456 | tf_op jit(solution)/shard_map/add | solution.py:41
  229.7 16.8 %rev.18 = f32[1,512,1024]{2,1,0:T(8,128)} reverse(f32[1,512,1024]{2,1,0:T(8,128)} %add.502), dimensions={1} | reverse | bytes 4194304 | tf_op jit(solution)/shard_map/rev | solution.py:41
  246.5 30.6 %all_gather.14 = f32[8,1,1024]{2,1,0:T(1,128)S(1)} all-gather(f32[1,1,1024]{2,1,0:T(1,128)S(1)} %slice_add_fusion.1), channel_id=1, replica_groups=mesh['sp'=8,'tp'=4] {'sp'}, dimensions={0}, use_global_device_ids=true | all-gather | bytes 36864 | tf_op jit(solution)/shard_map/all_gather | solution.py:9
  277.1 4.8 %pad.273 = f32[1,512,1024]{2,1,0:T(8,128)} pad(f32[1,256,1024]{2,1,0:T(8,128)S(1)} %copy-done.5, f32[]{:T(128)} %constant.61.clone.1), padding=0_0_0x1_0_1x0_0_0 | pad | bytes 3145732 | tf_op jit(solution)/shard_map/pad | solution.py:41
  282.7 3.3 add.493
  286.0 16.8 %rev.17 = f32[1,512,1024]{2,1,0:T(8,128)} reverse(f32[1,512,1024]{2,1,0:T(8,128)} %add.493), dimensions={1} | reverse | bytes 4194304 | tf_op jit(solution)/shard_map/rev | solution.py:41
  302.8 30.6 %all_gather.15 = f32[8,1,1024]{2,1,0:T(1,128)S(1)} all-gather(f32[1,1,1024]{2,1,0:T(1,128)S(1)} %slice_add_fusion), channel_id=1, replica_groups=mesh['sp'=8,'tp'=4] {'sp'}, dimensions={0}, use_global_device_ids=true | all-gather | bytes 36864 | tf_op jit(solution)/shard_map/all_gather | solution.py:9
  333.7 6.5 %multiply_reduce_fusion = (f32[512]{0:T(512)S(1)}, f32[1,512,1024]{2,1,0:T(8,128)}) fusion(bf16[1,512,1024]{2,1,0:T(8,128)(2,1)S(1)} %copy-done.14, f32[1,512,1024]{2,1,0:T(8,128)} %rev.17, f32[1,512,1024]{2,1,0:T(8,128)} %rev.18, f32[1024]{0:T(1024)S(1)} %bitcast.28, f32[1024]{0:T(1024)S(1)} %bitcast.29, f32[1,512,1024]{2,1,0:T(8,128)S(1)} %copy-done.3, ...), kind=kLoop, calls=%fused_computation.9 | loop fusion | flops 7339520 | bytes 15738880 | tf_op jit(solution)/shard_map/reduce_sum | solution.py:52
  340.2 5.6 %psum.7 = f32[1,512,1]{1,2,0:T(1,128)S(1)} all-reduce(f32[1,512,1]{1,2,0:T(1,128)S(1)} %bitcast.31), channel_id=1, replica_groups=mesh['sp'=8,'tp'=4] {'tp'}, use_global_device_ids=true, to_apply=%region_5.6 | all-reduce | flops 512 | bytes 4096 | tf_op jit(solution)/shard_map/psum | solution.py:52
  345.9 2.8 multiply_convert_fusion
  (302 shorter events, 27.9 us)
Async XLA Ops:
  51.0 2.9 copy-start.9
  51.0 2.9 copy-start.10
  59.3 1.0 copy-start.11
  69.4 2.6 copy-start
  75.8 55.5 %copy-start.2 = (f32[1,512,1024]{2,1,0:T(8,128)}, f32[1,512,1024]{2,1,0:T(8,128)S(1)}, u32[]{:S(2)}) copy-start(f32[1,512,1024]{2,1,0:T(8,128)S(1)} %pad.254) | copy-start | bytes 6291460
  75.8 8.8 %copy-start.6 = (f32[1,256,1024]{2,1,0:T(8,128)S(1)}, f32[1,256,1024]{2,1,0:T(8,128)}, u32[]{:S(2)}) copy-start(f32[1,256,1024]{2,1,0:T(8,128)} %add.455) | copy-start | bytes 3145732
  89.5 73.7 %copy-start.4 = (bf16[1,512,1024]{2,1,0:T(8,128)(2,1)S(1)}, bf16[1,512,1024]{2,1,0:T(8,128)(2,1)}, u32[]{:S(2)}) copy-start(bf16[1,512,1024]{2,1,0:T(8,128)(2,1)} %param.9) | copy-start | bytes 3145732
  178.6 5.7 %copy-start.8 = (f32[1,256,1024]{2,1,0:T(8,128)S(1)}, f32[1,256,1024]{2,1,0:T(8,128)}, u32[]{:S(2)}) copy-start(f32[1,256,1024]{2,1,0:T(8,128)} %slice.633) | copy-start | bytes 3145732
  194.5 1.0 copy-start.12
  194.5 1.2 copy-start.13
  204.8 2.6 copy-start.1
  211.2 8.7 %copy-start.7 = (f32[1,256,1024]{2,1,0:T(8,128)S(1)}, f32[1,256,1024]{2,1,0:T(8,128)}, u32[]{:S(2)}) copy-start(f32[1,256,1024]{2,1,0:T(8,128)} %add.501) | copy-start | bytes 3145732
  229.7 47.4 %copy-start.5 = (f32[1,256,1024]{2,1,0:T(8,128)S(1)}, f32[1,256,1024]{2,1,0:T(8,128)}, u32[]{:S(2)}) copy-start(f32[1,256,1024]{2,1,0:T(8,128)} %add.491) | copy-start | bytes 3145732
  286.0 47.7 %copy-start.3 = (f32[1,512,1024]{2,1,0:T(8,128)S(1)}, f32[1,512,1024]{2,1,0:T(8,128)}, u32[]{:S(2)}) copy-start(f32[1,512,1024]{2,1,0:T(8,128)} %copy-done.2) | copy-start | bytes 6291460
  286.0 47.7 %copy-start.14 = (bf16[1,512,1024]{2,1,0:T(8,128)(2,1)S(1)}, bf16[1,512,1024]{2,1,0:T(8,128)(2,1)}, u32[]{:S(2)}) copy-start(bf16[1,512,1024]{2,1,0:T(8,128)(2,1)} %param.10) | copy-start | bytes 3145732
  333.7 12.2 %copy-start.15 = (f32[1024]{0:T(1024)S(1)}, f32[1024]{0:T(1024)}, u32[]{:S(2)}) copy-start(f32[1024]{0:T(1024)} %param.11) | copy-start | bytes 12292
where the time goes:
time: 353 us; the launch traced here: 349 us
  local copies, waits for them, and re-layouts  167 us (47%)
  blocking collectives  130 us (37%)
  other arithmetic  49.3 us (14%)
    all_gather x4, blocking collectives, prefix(): pieces = jax.tree.map(lambda part: lax.all_gather(part, axis), value)  124 us
    slice x60, local copies, waits for them, and re-layouts, body(): lax.associative_scan(join_pair, (keep, push), axis=1, reverse=True)  40.6 us
    rev x2, local copies, waits for them, and re-layouts, body(): lax.associative_scan(join_pair, (keep, push), axis=1, reverse=True)  33.6 us
    pad x32, local copies, waits for them, and re-layouts, body(): product, forward = lax.associative_scan(join_pair, (keep, push), axis=1)  30.2 us
    pad x32, local copies, waits for them, and re-layouts, body(): lax.associative_scan(join_pair, (keep, push), axis=1, reverse=True)  26.3 us
    slice x60, local copies, waits for them, and re-layouts, body(): product, forward = lax.associative_scan(join_pair, (keep, push), axis=1)  24.5 us
    add x19, other arithmetic, body(): lax.associative_scan(join_pair, (keep, push), axis=1, reverse=True)  13.1 us
    another operation x1, local copies, waits for them, and re-layouts  10.7 us

commit v1 on v0

v1 whole, which is shorter than its diff:
```python
import functools

import jax
import jax.numpy as jnp
from jax import lax
from jax.experimental import pallas as pl
from jax.experimental.pallas import tpu as pltpu
from jax.sharding import PartitionSpec as P

LANES = 128
SEGMENTS = 8


def totals_kernel(scale, root, decay_ref, drive_ref, own_ref, prod_ref, first_ref, last_ref, rate_ref, push_ref):
    rows, width = decay_ref.shape
    steps = rows // SEGMENTS
    tiles = width // LANES

    def spread(m, _):
        for s in range(SEGMENTS):
            src = pl.ds(pl.multiple_of(s * steps + m * 16, 16), 16)
            for j in range(tiles):
                lanes = pl.ds(j * LANES, LANES)
                decay = decay_ref[src, lanes] * scale
                push = drive_ref[src, lanes].astype(jnp.float32) * root
                for h in range(2):
                    dst = pl.ds(j * rows + m * 16 * SEGMENTS + h * 8 * SEGMENTS + s, 8, stride=SEGMENTS)
                    rate_ref[dst, :] = decay[h * 8 : h * 8 + 8]
                    push_ref[dst, :] = push[h * 8 : h * 8 + 8]
        return 0

    lax.fori_loop(0, steps // 16, spread, 0)

    def step(i, carry):
        out = []
        for j in range(tiles):
            prod, fwd, bwd = carry[j]
            at = pl.ds(pl.multiple_of(j * rows + i * SEGMENTS, SEGMENTS), SEGMENTS)
            keep = jnp.exp(-rate_ref[at, :])
            push = push_ref[at, :]
            bwd = bwd + prod * push
            fwd = keep * fwd + push
            prod = prod * keep
            out.append((prod, fwd, bwd))
        return tuple(out)

    one = jnp.ones((SEGMENTS, LANES), jnp.float32)
    zero = jnp.zeros((SEGMENTS, LANES), jnp.float32)
    carry = lax.fori_loop(0, steps, step, ((one, zero, zero),) * tiles, unroll=8)
    for j in range(tiles):
        lanes = pl.ds(j * LANES, LANES)
        prod, fwd, bwd = carry[j]
        prod_ref[:, lanes] = prod
        first_ref[:, lanes] = fwd
        last_ref[:, lanes] = bwd
        p, f, b = prod[0:1], fwd[0:1], bwd[0:1]
        for s in range(1, SEGMENTS):
            b = b + p * bwd[s : s + 1]
            f = prod[s : s + 1] * f + fwd[s : s + 1]
            p = p * prod[s : s + 1]
        own_ref[0:1, lanes] = p
        own_ref[1:2, lanes] = f
        own_ref[2:3, lanes] = b
        own_ref[3:4, lanes] = jnp.zeros_like(b)


def states_kernel(mine_ref, all_ref, prod_ref, first_ref, last_ref, rate_ref, push_ref, gate_ref, gated_ref, power_ref, ent_ref, acc_ref, state_ref):
    rows, width = gate_ref.shape
    steps = rows // SEGMENTS
    tiles = width // LANES
    count = all_ref.shape[0]
    mine = mine_ref[0]
    fwd = jnp.zeros((1, width), jnp.float32)
    bwd = jnp.zeros((1, width), jnp.float32)
    for n in range(count):
        fwd = jnp.where(n < mine, all_ref[n, 0:1, :] * fwd + all_ref[n, 1:2, :], fwd)
    for n in range(count - 1, -1, -1):
        bwd = jnp.where(n > mine, all_ref[n, 0:1, :] * bwd + all_ref[n, 2:3, :], bwd)
    for s in range(SEGMENTS):
        ent_ref[0, s : s + 1, :] = fwd
        fwd = prod_ref[s : s + 1, :] * fwd + first_ref[s : s + 1, :]
    for s in range(SEGMENTS - 1, -1, -1):
        bwd = prod_ref[s : s + 1, :] * bwd + last_ref[s : s + 1, :]
        ent_ref[1, s : s + 1, :] = bwd

    group = 4 if tiles % 4 == 0 else 1
    for g in range(0, tiles, group):

        def step(i, carry):
            out = []
            for j in range(group):
                f, b = carry[j]
                at = pl.ds(pl.multiple_of((g + j) * rows + i * SEGMENTS, SEGMENTS), SEGMENTS)
                x = rate_ref[at, :]
                push = push_ref[at, :]
                f = jnp.exp(-x) * f + push
                state_ref[at, :] = f + b
                b = (b - push) * jnp.exp(x)
                out.append((f, b))
            return tuple(out)

        start = tuple(
            (ent_ref[0, :, pl.ds((g + j) * LANES, LANES)], ent_ref[1, :, pl.ds((g + j) * LANES, LANES)])
            for j in range(group)
        )
        lax.fori_loop(0, steps, step, start, unroll=8)

    def gating(m, _):
        for s in range(SEGMENTS):
            at = pl.ds(pl.multiple_of(s * steps + m * 16, 16), 16)
            acc = jnp.zeros((16, LANES), jnp.float32)
            for j in range(tiles):
                lanes = pl.ds(j * LANES, LANES)
                base = j * rows + m * 16 * SEGMENTS + s
                half = [state_ref[pl.ds(base + h * 8 * SEGMENTS, 8, stride=SEGMENTS), :] for h in range(2)]
                g = jnp.concatenate(half, axis=0) / (1.0 + jnp.exp(-gate_ref[at, lanes].astype(jnp.float32)))
                gated_ref[at, lanes] = g
                acc = acc + g * g
            acc_ref[at, :] = acc
        return 0

    lax.fori_loop(0, steps // 16, gating, 0)
    for r in range(rows // LANES):
        block = acc_ref[r * LANES : (r + 1) * LANES, :].T
        power_ref[r : r + 1, :] = jnp.sum(block, axis=0, keepdims=True)


def norm_kernel(channels, power_ref, gain_ref, gated_ref, out_ref):
    rows, width = gated_ref.shape
    for r in range(rows // LANES):
        total = power_ref[0, pl.ds(r, 1), :]
        for n in range(1, power_ref.shape[0]):
            total = total + power_ref[n, pl.ds(r, 1), :]
        factor = lax.rsqrt(total / channels + 1e-06)
        factor = jnp.broadcast_to(factor, (LANES, LANES)).T
        at = slice(r * LANES, (r + 1) * LANES)
        for j in range(width // LANES):
            lanes = slice(j * LANES, (j + 1) * LANES)
            out_ref[at, lanes] = (gated_ref[at, lanes] * factor * gain_ref[:, lanes]).astype(jnp.bfloat16)


def body(decay_rate, drive_in, gate_in, norm_gain):
    batch, rows, width = decay_rate.shape
    length = rows * lax.axis_size("sp")
    channels = width * lax.axis_size("tp")
    f32 = jnp.float32
    decay = decay_rate.reshape(rows, width)
    drive = drive_in.reshape(rows, width)
    gate = gate_in.reshape(rows, width)
    block = min(width, 256)
    vmem = pl.BlockSpec(memory_space=pltpu.VMEM)
    cols = lambda r: pl.BlockSpec((r, block), lambda c: (0, c))
    stack = pl.BlockSpec((rows * block // LANES, LANES), lambda c: (c, 0))
    own, prod, first, last, rate, push = pl.pallas_call(
        functools.partial(totals_kernel, 1.0 / length, length ** (-0.5)),
        grid=(width // block,),
        in_specs=[cols(rows), cols(rows)],
        out_specs=[cols(4), cols(SEGMENTS), cols(SEGMENTS), cols(SEGMENTS), stack, stack],
        out_shape=[jax.ShapeDtypeStruct((4, width), f32)]
        + [jax.ShapeDtypeStruct((SEGMENTS, width), f32)] * 3
        + [jax.ShapeDtypeStruct((rows * width // LANES, LANES), f32)] * 2,
        name="totals",
    )(decay, drive)
    everyone = lax.all_gather(own, "sp")
    mine = lax.axis_index("sp").astype(jnp.int32).reshape(1)
    gated, power = pl.pallas_call(
        states_kernel,
        in_specs=[pl.BlockSpec(memory_space=pltpu.SMEM)] + [vmem] * 7,
        out_specs=[vmem, vmem],
        out_shape=[jax.ShapeDtypeStruct((rows, width), f32), jax.ShapeDtypeStruct((rows // LANES, LANES), f32)],
        scratch_shapes=[pltpu.VMEM((2, SEGMENTS, width), f32), pltpu.VMEM((rows, LANES), f32), pltpu.VMEM((rows * width // LANES, LANES), f32)],
        name="states",
    )(mine, everyone, prod, first, last, rate, push, gate)
    powers = lax.all_gather(power, "tp")
    filtered = pl.pallas_call(
        functools.partial(norm_kernel, float(channels)),
        in_specs=[vmem, vmem, vmem],
        out_specs=vmem,
        out_shape=jax.ShapeDtypeStruct((rows, width), jnp.bfloat16),
        name="norm",
    )(powers, norm_gain.reshape(1, width), gated)
    return filtered.reshape(batch, rows, width)


def solution(mesh):
    in_specs = (P(None, "sp", "tp"), P(None, "sp", "tp"), P(None, "sp", "tp"), P("tp"))
    out_specs = P(None, "sp", "tp")
    return jax.shard_map(body, mesh=mesh, in_specs=in_specs, out_specs=out_specs, check_vma=False)
```

time: 353 us -> 55.1 us (0.16); the launches traced: 349 us -> 54.9 us
  local copies, waits for them, and re-layouts: 167 us -> 0 us
  blocking collectives: 130 us -> 41.1 us
  other arithmetic: 49.3 us -> 0 us
  Pallas kernels: 0 us -> 13.8 us
    all_gather x4 -> x2, blocking collectives: 124 us -> 41.1 us  [the longest x1 34.5 us: body(): everyone = lax.all_gather(own, 'sp')]
    slice x120 -> x0, local copies, waits for them, and re-layouts: 65.1 us -> none  [the longest x60 40.6 us: body(): lax.associative_scan(join_pair, (keep, push), axis=1, reverse=True)]
    pad x64 -> x0, local copies, waits for them, and re-layouts: 56.5 us -> none  [the longest x32 30.2 us: body(): product, forward = lax.associative_scan(join_pair, (keep, push), axis=1)]
    rev x4 -> x0, local copies, waits for them, and re-layouts: 33.6 us -> none  [the longest x2 33.6 us: body(): lax.associative_scan(join_pair, (keep, push), axis=1, reverse=True)]
    add x51 -> x0, other arithmetic: 25.7 us -> none  [the longest x19 13.1 us: body(): lax.associative_scan(join_pair, (keep, push), axis=1, reverse=True)]
    pallas_call x0 -> x3, Pallas kernels: none -> 13.8 us  [the longest x1 5.59 us: body(): pl.pallas_call(states_kernel, in_specs=[pl.BlockSpec(memory_space=pltpu.S...]
    another operation x1 -> x0, local copies, waits for them, and re-layouts: 10.7 us -> none
    mul x17 -> x0, other arithmetic: 7.24 us -> none  [the longest x16 5.76 us: join_pair(): return (earlier[0] * later[0], later[0] * earlier[1] + later[1])]
where the time goes in v1:
time: 55.1 us; the launch traced here: 54.9 us
  blocking collectives  41.1 us (75%)
  Pallas kernels  13.8 us (25%)
    all_gather x1, blocking collectives, body(): everyone = lax.all_gather(own, 'sp')  34.5 us
    all_gather x1, blocking collectives, body(): powers = lax.all_gather(power, 'tp')  6.51 us
    pallas_call x1, Pallas kernels, body(): pl.pallas_call(states_kernel, in_specs=[pl.BlockSpec(memory_space=pltpu.S...  5.59 us
    pallas_call x1, Pallas kernels, body(): pl.pallas_call(functools.partial(totals_kernel, 1.0 / length, length ** (...  5.34 us
    pallas_call x1, Pallas kernels, body(): pl.pallas_call(functools.partial(norm_kernel, float(channels)), in_specs=...  2.91 us

profile of v1, /device:TPU:0, one launch (start us, length us, event | category | flops | bytes accessed | tf_op | source)
XLA Modules:
  0.0 54.9 jit_solution(13805160086527008436)
XLA Ops:
  0.0 5.3 %totals.1 = (f32[4,1024]{1,0:T(4,128)}, f32[8,1024]{1,0:T(8,128)}, f32[8,1024]{1,0:T(8,128)}, f32[8,1024]{1,0:T(8,128)}, f32[4096,128]{1,0:T(8,128)}, /*index=5*/f32[4096,128]{1,0:T(8,128)}) custom-call(f32[512,1024]{1,0:T(8,128)} %bitcast.8, bf16[512,1024]{1,0:T(8,128)(2,1)} %bitcast.9), custom_call_target="tpu_custom_call" | custom-call | tf_op jit(solution)/shard_map/totals/pallas_call | solution.py:154
  5.3 34.5 %all-gather.2.all_ref = f32[8,4,1024]{2,1,0:T(4,128)} all-gather(f32[1,4,1024]{2,1,0:T(4,128)} %bitcast.11), channel_id=2, replica_groups=mesh['sp'=8,'tp'=4] {'sp'}, dimensions={0}, use_global_device_ids=true | all-gather | bytes 147456 | tf_op jit(solution)/shard_map/all_gather | solution.py:164
  39.9 5.6 %states.1 = (f32[512,1024]{1,0:T(8,128)}, f32[4,128]{1,0:T(4,128)}) custom-call(s32[1]{0:T(128)} %bitcast.mine_ref, f32[8,4,1024]{2,1,0:T(4,128)} %all-gather.2.all_ref, f32[8,1024]{1,0:T(8,128)} %get-tuple-element.14.prod_ref, f32[8,1024]{1,0:T(8,128)} %get-tuple-element.15.first_ref, f32[8,1024]{1,0:T(8,128)} %get-tuple-element.16.last_ref, ...), custom_call_target="tpu_custom_call" | custom-call | tf_op jit(solution)/shard_map/states/pallas_call | solution.py:166
  45.5 6.5 %all-gather.3.power_ref = f32[4,4,128]{2,1,0:T(4,128)} all-gather(f32[1,4,128]{2,1,0:T(4,128)} %bitcast.13), channel_id=3, replica_groups=mesh['sp'=8,'tp'=4] {'tp'}, dimensions={0}, use_global_device_ids=true | all-gather | bytes 10240 | tf_op jit(solution)/shard_map/all_gather | solution.py:174
  52.0 2.9 %norm.1 = bf16[512,1024]{1,0:T(8,128)(2,1)} custom-call(f32[4,4,128]{2,1,0:T(4,128)} %all-gather.3.power_ref, f32[1,1024]{1,0:T(1,128)} %bitcast.12, f32[512,1024]{1,0:T(8,128)} %get-tuple-element.20.gated_ref), custom_call_target="tpu_custom_call" | custom-call | tf_op jit(solution)/shard_map/norm/pallas_call | solution.py:175

commit v2 on v1

--- a/solution.py
+++ b/solution.py
@@ -58,10 +58,11 @@
             b = b + p * bwd[s : s + 1]
             f = prod[s : s + 1] * f + fwd[s : s + 1]
             p = p * prod[s : s + 1]
-        own_ref[0:1, lanes] = p
-        own_ref[1:2, lanes] = f
-        own_ref[2:3, lanes] = b
-        own_ref[3:4, lanes] = jnp.zeros_like(b)
+        for n in range(own_ref.shape[0]):
+            own_ref[n, 0:1, lanes] = p
+            own_ref[n, 1:2, lanes] = f
+            own_ref[n, 2:3, lanes] = b
+            own_ref[n, 3:4, lanes] = jnp.zeros_like(b)
 
 
 def states_kernel(mine_ref, all_ref, prod_ref, first_ref, last_ref, rate_ref, push_ref, gate_ref, gated_ref, power_ref, ent_ref, acc_ref, state_ref):
@@ -122,21 +123,27 @@
     lax.fori_loop(0, steps // 16, gating, 0)
     for r in range(rows // LANES):
         block = acc_ref[r * LANES : (r + 1) * LANES, :].T
-        power_ref[r : r + 1, :] = jnp.sum(block, axis=0, keepdims=True)
+        power = jnp.sum(block, axis=0, keepdims=True)
+        for n in range(power_ref.shape[0]):
+            power_ref[n, r : r + 1, :] = power
 
 
 def norm_kernel(channels, power_ref, gain_ref, gated_ref, out_ref):
     rows, width = gated_ref.shape
     for r in range(rows // LANES):
-        total = power_ref[0, pl.ds(r, 1), :]
+        total = power_ref[0, r : r + 1, :]
         for n in range(1, power_ref.shape[0]):
-            total = total + power_ref[n, pl.ds(r, 1), :]
+            total = total + power_ref[n, r : r + 1, :]
         factor = lax.rsqrt(total / channels + 1e-06)
         factor = jnp.broadcast_to(factor, (LANES, LANES)).T
         at = slice(r * LANES, (r + 1) * LANES)
         for j in range(width // LANES):
             lanes = slice(j * LANES, (j + 1) * LANES)
             out_ref[at, lanes] = (gated_ref[at, lanes] * factor * gain_ref[:, lanes]).astype(jnp.bfloat16)
+
+
+def held(value):
+    return pltpu.with_memory_space_constraint(value, pltpu.VMEM)
 
 
 def body(decay_rate, drive_in, gate_in, norm_gain):
@@ -155,30 +162,30 @@
         functools.partial(totals_kernel, 1.0 / length, length ** (-0.5)),
         grid=(width // block,),
         in_specs=[cols(rows), cols(rows)],
-        out_specs=[cols(4), cols(SEGMENTS), cols(SEGMENTS), cols(SEGMENTS), stack, stack],
-        out_shape=[jax.ShapeDtypeStruct((4, width), f32)]
-        + [jax.ShapeDtypeStruct((SEGMENTS, width), f32)] * 3
+        out_specs=[pl.BlockSpec((lax.axis_size("sp"), 4, block), lambda c: (0, 0, c)), cols(SEGMENTS), cols(SEGMENTS), cols(SEGMENTS), stack, stack],
+        out_shape=[pltpu.VMEM((lax.axis_size("sp"), 4, width), f32)]
+        + [pltpu.VMEM((SEGMENTS, width), f32)] * 3
         + [jax.ShapeDtypeStruct((rows * width // LANES, LANES), f32)] * 2,
         name="totals",
     )(decay, drive)
-    everyone = lax.all_gather(own, "sp")
+    others = held(lax.all_to_all(own, "sp", 0, 0, tiled=True))
     mine = lax.axis_index("sp").astype(jnp.int32).reshape(1)
     gated, power = pl.pallas_call(
         states_kernel,
         in_specs=[pl.BlockSpec(memory_space=pltpu.SMEM)] + [vmem] * 7,
         out_specs=[vmem, vmem],
-        out_shape=[jax.ShapeDtypeStruct((rows, width), f32), jax.ShapeDtypeStruct((rows // LANES, LANES), f32)],
+        out_shape=[pltpu.VMEM((rows, width), f32), pltpu.VMEM((lax.axis_size("tp"), rows // LANES, LANES), f32)],
         scratch_shapes=[pltpu.VMEM((2, SEGMENTS, width), f32), pltpu.VMEM((rows, LANES), f32), pltpu.VMEM((rows * width // LANES, LANES), f32)],
         name="states",
-    )(mine, everyone, prod, first, last, rate, push, gate)
-    powers = lax.all_gather(power, "tp")
+    )(mine, others, held(prod), held(first), held(last), rate, push, gate)
+    powers = held(lax.all_to_all(power, "tp", 0, 0, tiled=True))
     filtered = pl.pallas_call(
         functools.partial(norm_kernel, float(channels)),
-        in_specs=[vmem, vmem, vmem],
+        in_specs=[vmem] * 3,
         out_specs=vmem,
         out_shape=jax.ShapeDtypeStruct((rows, width), jnp.bfloat16),
         name="norm",
-    )(powers, norm_gain.reshape(1, width), gated)
+    )(powers, norm_gain.reshape(1, width), held(gated))
     return filtered.reshape(batch, rows, width)
 
 

time: 55.1 us -> 36 us (0.65)
  blocking collectives: 41.1 us -> 6.36 us
  waiting for transfers between devices: 0 us -> 7.34 us
  starting transfers between devices: 0 us -> 7.31 us
  local copies, waits for them, and re-layouts: 0 us -> 2.92 us
  Pallas kernels: 13.8 us -> 11.6 us
    all_gather x2 -> x0, blocking collectives: 41.1 us -> none  [the longest x1 34.5 us: body(): everyone = lax.all_gather(own, 'sp')]
    all_to_all x0 -> x1, waiting for transfers between devices: none -> 7.34 us  [body(): others = held(lax.all_to_all(own, 'sp', 0, 0, tiled=True))]
    all_to_all x0 -> x1, starting transfers between devices: none -> 7.31 us  [body(): others = held(lax.all_to_all(own, 'sp', 0, 0, tiled=True))]
    all_to_all x0 -> x1, blocking collectives: none -> 6.36 us  [body(): powers = held(lax.all_to_all(power, 'tp', 0, 0, tiled=True))]
    unnamed x0 -> x4, local copies, waits for them, and re-layouts: none -> 2.92 us
    pallas_call x1, Pallas kernels: 5.59 us -> 4.34 us  [body(): pl.pallas_call(states_kernel, in_specs=[pl.BlockSpec(memory_space=pltpu.S...]
    pallas_call x1, Pallas kernels: 2.91 us -> 1.97 us  [body(): pl.pallas_call(functools.partial(norm_kernel, float(channels)), in_specs=...]
  transfers between devices with their start and end apart: 0 -> 1, of which waited for: 0 -> 1; matrix products, arithmetic and copies ran while one was open for 0% -> 0% of each run, Pallas kernels for 0% -> 0%
where the time goes in v2:
time: 36 us; the launch traced here: 35.6 us
  Pallas kernels  11.6 us (32%)
  waiting for transfers between devices  7.34 us (20%)
  starting transfers between devices  7.31 us (20%)
  blocking collectives  6.36 us (18%)
  local copies, waits for them, and re-layouts  2.92 us (8%)
    all_to_all x1, waiting for transfers between devices, body(): others = held(lax.all_to_all(own, 'sp', 0, 0, tiled=True))  7.34 us
    all_to_all x1, starting transfers between devices, body(): others = held(lax.all_to_all(own, 'sp', 0, 0, tiled=True))  7.31 us
    all_to_all x1, blocking collectives, body(): powers = held(lax.all_to_all(power, 'tp', 0, 0, tiled=True))  6.36 us
    pallas_call x1, Pallas kernels, body(): pl.pallas_call(functools.partial(totals_kernel, 1.0 / length, length ** (...  5.34 us
    pallas_call x1, Pallas kernels, body(): pl.pallas_call(states_kernel, in_specs=[pl.BlockSpec(memory_space=pltpu.S...  4.34 us
    unnamed x4, local copies, waits for them, and re-layouts  2.92 us
    pallas_call x1, Pallas kernels, body(): pl.pallas_call(functools.partial(norm_kernel, float(channels)), in_specs=...  1.97 us
  transfers between devices with their start and end apart: 1, of which 1 were waited for; matrix products, arithmetic and copies ran while one was open for 0% of the time, Pallas kernels for 0%

profile of v2, /device:TPU:0, one launch (start us, length us, event | category | flops | bytes accessed | tf_op | source)
XLA Modules:
  0.0 35.6 jit_solution(6605891733520665037)
XLA Ops:
  0.0 5.3 %totals.1 = (f32[8,4,1024]{2,1,0:T(4,128)}, f32[8,1024]{1,0:T(8,128)S(1)}, f32[8,1024]{1,0:T(8,128)S(1)}, f32[8,1024]{1,0:T(8,128)S(1)}, f32[4096,128]{1,0:T(8,128)}, /*index=5*/f32[4096,128]{1,0:T(8,128)}) custom-call(f32[512,1024]{1,0:T(8,128)} %bitcast.6, bf16[512,1024]{1,0:T(8,128)(2,1)} %bitcast.7), custom_call_target="tpu_custom_call" | custom-call | tf_op jit(solution)/shard_map/totals/pallas_call | solution.py:161
  5.3 7.3 %all-to-all-start = ((f32[8,4,1024]{2,1,0:T(4,128)}), f32[8,4,1024]{2,1,0:T(4,128)S(1)}, u32[]{:S(2)}, u32[]{:S(2)}) async-start(f32[8,4,1024]{2,1,0:T(4,128)} %get-tuple-element.13), calls=%async_computation | async-start | bytes 262144 | tf_op jit(solution)/shard_map/all_to_all | solution.py:171
  12.6 7.3 %all-to-all-done.all_ref = f32[8,4,1024]{2,1,0:T(4,128)S(1)} async-done(((f32[8,4,1024]{2,1,0:T(4,128)}), f32[8,4,1024]{2,1,0:T(4,128)S(1)}, u32[]{:S(2)}, u32[]{:S(2)}) %all-to-all-start) | async-done | bytes 131104 | tf_op jit(solution)/shard_map/all_to_all | solution.py:171
  20.0 4.3 %states.1 = (f32[512,1024]{1,0:T(8,128)S(1)}, f32[4,4,128]{2,1,0:T(4,128)S(1)}) custom-call(s32[1]{0:T(128)} %bitcast.mine_ref, f32[8,4,1024]{2,1,0:T(4,128)S(1)} %all-to-all-done.all_ref, f32[8,1024]{1,0:T(8,128)S(1)} %get-tuple-element.14.prod_ref, f32[8,1024]{1,0:T(8,128)S(1)} %get-tuple-element.15.first_ref, f32[8,1024]{1,0:T(8,128)S(1)} %get-tuple-element.16.last_ref, ...), custom_call_target="tpu_custom_call" | custom-call | tf_op jit(solution)/shard_map/states/pallas_call | solution.py:173
  24.3 0.0 copy-start
  24.3 1.3 %copy-done = f32[512,1024]{1,0:T(8,128)} copy-done((f32[512,1024]{1,0:T(8,128)}, f32[512,1024]{1,0:T(8,128)S(1)}, u32[]{:S(2)}) %copy-start) | copy-done | bytes 2097176
  25.7 6.4 %all_to_all.10.power_ref = f32[4,4,128]{2,1,0:T(4,128)S(1)} all-to-all(f32[4,4,128]{2,1,0:T(4,128)S(1)} %get-tuple-element.19), channel_id=1, replica_groups=mesh['sp'=8,'tp'=4] {'tp'}, dimensions={0} | all-to-all | bytes 16384 | tf_op jit(solution)/shard_map/all_to_all | solution.py:181
  32.0 0.0 copy-start.1
  32.0 1.6 %copy-done.1 = f32[512,1024]{1,0:T(8,128)S(1)} copy-done((f32[512,1024]{1,0:T(8,128)S(1)}, f32[512,1024]{1,0:T(8,128)}, u32[]{:S(2)}) %copy-start.1) | copy-done | bytes 2097176
  33.6 2.0 %norm.1 = bf16[512,1024]{1,0:T(8,128)(2,1)} custom-call(f32[4,4,128]{2,1,0:T(4,128)S(1)} %all_to_all.10.power_ref, f32[1,1024]{1,0:T(1,128)} %bitcast.9, f32[512,1024]{1,0:T(8,128)S(1)} %copy-done.1), custom_call_target="tpu_custom_call" | custom-call | tf_op jit(solution)/shard_map/norm/pallas_call | solution.py:182
Async XLA Ops:
  5.3 14.7 %all-to-all-start = ((f32[8,4,1024]{2,1,0:T(4,128)}), f32[8,4,1024]{2,1,0:T(4,128)S(1)}, u32[]{:S(2)}, u32[]{:S(2)}) async-start(f32[8,4,1024]{2,1,0:T(4,128)} %get-tuple-element.13), calls=%async_computation | async-start | bytes 262144 | tf_op jit(solution)/shard_map/all_to_all | solution.py:171
  24.3 1.3 %copy-start = (f32[512,1024]{1,0:T(8,128)}, f32[512,1024]{1,0:T(8,128)S(1)}, u32[]{:S(2)}) copy-start(f32[512,1024]{1,0:T(8,128)S(1)} %get-tuple-element.20.gated_ref) | copy-start | bytes 6291460
  32.0 1.6 %copy-start.1 = (f32[512,1024]{1,0:T(8,128)S(1)}, f32[512,1024]{1,0:T(8,128)}, u32[]{:S(2)}) copy-start(f32[512,1024]{1,0:T(8,128)} %copy-done) | copy-start | bytes 6291460

commit v3 on v2

--- a/solution.py
+++ b/solution.py
@@ -11,15 +11,14 @@
 SEGMENTS = 8
 
 
-def totals_kernel(scale, root, decay_ref, drive_ref, own_ref, prod_ref, first_ref, last_ref, rate_ref, push_ref):
+def spread(scale, root, decay_ref, drive_ref, rate_ref, push_ref):
     rows, width = decay_ref.shape
     steps = rows // SEGMENTS
-    tiles = width // LANES
-
-    def spread(m, _):
+
+    def some(m, _):
         for s in range(SEGMENTS):
             src = pl.ds(pl.multiple_of(s * steps + m * 16, 16), 16)
-            for j in range(tiles):
+            for j in range(width // LANES):
                 lanes = pl.ds(j * LANES, LANES)
                 decay = decay_ref[src, lanes] * scale
                 push = drive_ref[src, lanes].astype(jnp.float32) * root
@@ -29,7 +28,14 @@
                     push_ref[dst, :] = push[h * 8 : h * 8 + 8]
         return 0
 
-    lax.fori_loop(0, steps // 16, spread, 0)
+    lax.fori_loop(0, steps // 16, some, 0)
+
+
+def totals_kernel(scale, root, decay_ref, drive_ref, own_ref, prod_ref, first_ref, last_ref, rate_ref, push_ref):
+    rows, width = decay_ref.shape
+    steps = rows // SEGMENTS
+    tiles = width // LANES
+    spread(scale, root, decay_ref, drive_ref, rate_ref, push_ref)
 
     def step(i, carry):
         out = []
@@ -65,7 +71,13 @@
             own_ref[n, 3:4, lanes] = jnp.zeros_like(b)
 
 
-def states_kernel(mine_ref, all_ref, prod_ref, first_ref, last_ref, rate_ref, push_ref, gate_ref, gated_ref, power_ref, ent_ref, acc_ref, state_ref):
+def states_kernel(scale, root, mine_ref, all_ref, prod_ref, first_ref, last_ref, decay_ref, drive_ref, gate_ref, gated_ref, power_ref, ent_ref, acc_ref, state_ref, rate_ref, push_ref):
+    spread(scale, root, decay_ref, drive_ref, rate_ref, push_ref)
+
+    @pl.when(pl.program_id(0) == 0)
+    def _():
+        acc_ref[...] = jnp.zeros_like(acc_ref)
+
     rows, width = gate_ref.shape
     steps = rows // SEGMENTS
     tiles = width // LANES
@@ -84,7 +96,7 @@
         bwd = prod_ref[s : s + 1, :] * bwd + last_ref[s : s + 1, :]
         ent_ref[1, s : s + 1, :] = bwd
 
-    group = 4 if tiles % 4 == 0 else 1
+    group = tiles
     for g in range(0, tiles, group):
 
         def step(i, carry):
@@ -109,7 +121,7 @@
     def gating(m, _):
         for s in range(SEGMENTS):
             at = pl.ds(pl.multiple_of(s * steps + m * 16, 16), 16)
-            acc = jnp.zeros((16, LANES), jnp.float32)
+            acc = acc_ref[at, :]
             for j in range(tiles):
                 lanes = pl.ds(j * LANES, LANES)
                 base = j * rows + m * 16 * SEGMENTS + s
@@ -121,25 +133,25 @@
         return 0
 
     lax.fori_loop(0, steps // 16, gating, 0)
-    for r in range(rows // LANES):
-        block = acc_ref[r * LANES : (r + 1) * LANES, :].T
-        power = jnp.sum(block, axis=0, keepdims=True)
-        for n in range(power_ref.shape[0]):
-            power_ref[n, r : r + 1, :] = power
+    @pl.when(pl.program_id(0) == pl.num_programs(0) - 1)
+    def _():
+        for r in range(rows // LANES):
+            block = acc_ref[r * LANES : (r + 1) * LANES, :].T
+            power = jnp.sum(block, axis=0, keepdims=True)
+            for n in range(power_ref.shape[0]):
+                power_ref[n, r : r + 1, :] = power
 
 
 def norm_kernel(channels, power_ref, gain_ref, gated_ref, out_ref):
-    rows, width = gated_ref.shape
-    for r in range(rows // LANES):
-        total = power_ref[0, r : r + 1, :]
-        for n in range(1, power_ref.shape[0]):
-            total = total + power_ref[n, r : r + 1, :]
-        factor = lax.rsqrt(total / channels + 1e-06)
-        factor = jnp.broadcast_to(factor, (LANES, LANES)).T
-        at = slice(r * LANES, (r + 1) * LANES)
-        for j in range(width // LANES):
-            lanes = slice(j * LANES, (j + 1) * LANES)
-            out_ref[at, lanes] = (gated_ref[at, lanes] * factor * gain_ref[:, lanes]).astype(jnp.bfloat16)
+    r = pl.ds(pl.program_id(0), 1)
+    total = power_ref[0, r, :]
+    for n in range(1, power_ref.shape[0]):
+        total = total + power_ref[n, r, :]
+    factor = lax.rsqrt(total / channels + 1e-06)
+    factor = jnp.broadcast_to(factor, (LANES, LANES)).T
+    for j in range(gated_ref.shape[1] // LANES):
+        lanes = slice(j * LANES, (j + 1) * LANES)
+        out_ref[:, lanes] = (gated_ref[:, lanes] * factor * gain_ref[:, lanes]).astype(jnp.bfloat16)
 
 
 def held(value):
@@ -155,37 +167,53 @@
     drive = drive_in.reshape(rows, width)
     gate = gate_in.reshape(rows, width)
     block = min(width, 256)
-    vmem = pl.BlockSpec(memory_space=pltpu.VMEM)
     cols = lambda r: pl.BlockSpec((r, block), lambda c: (0, c))
-    stack = pl.BlockSpec((rows * block // LANES, LANES), lambda c: (c, 0))
-    own, prod, first, last, rate, push = pl.pallas_call(
-        functools.partial(totals_kernel, 1.0 / length, length ** (-0.5)),
+    scale, root = 1.0 / length, length ** (-0.5)
+    places, peers = lax.axis_size("sp"), lax.axis_size("tp")
+    stack = pltpu.VMEM((rows * block // LANES, LANES), f32)
+    whole = lambda shape: pl.BlockSpec(shape, lambda c: (0,) * len(shape))
+    whose = pl.BlockSpec((places, 4, block), lambda c: (0, 0, c))
+    own, prod, first, last = pl.pallas_call(
+        functools.partial(totals_kernel, scale, root),
         grid=(width // block,),
         in_specs=[cols(rows), cols(rows)],
-        out_specs=[pl.BlockSpec((lax.axis_size("sp"), 4, block), lambda c: (0, 0, c)), cols(SEGMENTS), cols(SEGMENTS), cols(SEGMENTS), stack, stack],
-        out_shape=[pltpu.VMEM((lax.axis_size("sp"), 4, width), f32)]
-        + [pltpu.VMEM((SEGMENTS, width), f32)] * 3
-        + [jax.ShapeDtypeStruct((rows * width // LANES, LANES), f32)] * 2,
+        out_specs=[whose, cols(SEGMENTS), cols(SEGMENTS), cols(SEGMENTS)],
+        out_shape=[pltpu.VMEM((places, 4, width), f32)] + [pltpu.VMEM((SEGMENTS, width), f32)] * 3,
+        scratch_shapes=[stack, stack],
         name="totals",
     )(decay, drive)
     others = held(lax.all_to_all(own, "sp", 0, 0, tiled=True))
     mine = lax.axis_index("sp").astype(jnp.int32).reshape(1)
     gated, power = pl.pallas_call(
-        states_kernel,
-        in_specs=[pl.BlockSpec(memory_space=pltpu.SMEM)] + [vmem] * 7,
-        out_specs=[vmem, vmem],
-        out_shape=[pltpu.VMEM((rows, width), f32), pltpu.VMEM((lax.axis_size("tp"), rows // LANES, LANES), f32)],
-        scratch_shapes=[pltpu.VMEM((2, SEGMENTS, width), f32), pltpu.VMEM((rows, LANES), f32), pltpu.VMEM((rows * width // LANES, LANES), f32)],
+        functools.partial(states_kernel, scale, root),
+        grid=(width // block,),
+        in_specs=[pl.BlockSpec(memory_space=pltpu.SMEM), whose]
+        + [cols(SEGMENTS)] * 3
+        + [cols(rows)] * 3,
+        out_specs=[cols(rows), whole((peers, rows // LANES, LANES))],
+        out_shape=[
+            jax.ShapeDtypeStruct((rows, width), f32),
+            pltpu.VMEM((peers, rows // LANES, LANES), f32),
+        ],
+        scratch_shapes=[
+            pltpu.VMEM((2, SEGMENTS, block), f32),
+            pltpu.VMEM((rows, LANES), f32),
+            stack,
+            stack,
+            stack,
+        ],
         name="states",
-    )(mine, others, held(prod), held(first), held(last), rate, push, gate)
+    )(mine, others, held(prod), held(first), held(last), decay, drive, gate)
     powers = held(lax.all_to_all(power, "tp", 0, 0, tiled=True))
+    span = pl.BlockSpec((LANES, width), lambda r: (r, 0))
     filtered = pl.pallas_call(
         functools.partial(norm_kernel, float(channels)),
-        in_specs=[vmem] * 3,
-        out_specs=vmem,
+        grid=(rows // LANES,),
+        in_specs=[whole((peers, rows // LANES, LANES)), whole((1, width)), span],
+        out_specs=span,
         out_shape=jax.ShapeDtypeStruct((rows, width), jnp.bfloat16),
         name="norm",
-    )(powers, norm_gain.reshape(1, width), held(gated))
+    )(powers, norm_gain.reshape(1, width), gated)
     return filtered.reshape(batch, rows, width)
 
 

time: 36 us -> 35.9 us (level)
  local copies, waits for them, and re-layouts: 2.92 us -> 0 us
  Pallas kernels: 11.6 us -> 14.4 us
    unnamed x4 -> x0, local copies, waits for them, and re-layouts: 2.92 us -> none
    pallas_call x3, Pallas kernels: 11.6 us -> 14.4 us  [the longest x1 6.1 us: body(): pl.pallas_call(functools.partial(states_kernel, scale, root), grid=(width...]
where the time goes in v3:
time: 35.9 us; the launch traced here: 35.5 us
  Pallas kernels  14.4 us (40%)
  waiting for transfers between devices  7.34 us (20%)
  starting transfers between devices  7.31 us (20%)
  blocking collectives  6.36 us (18%)
    all_to_all x1, waiting for transfers between devices, body(): others = held(lax.all_to_all(own, 'sp', 0, 0, tiled=True))  7.34 us
    all_to_all x1, starting transfers between devices, body(): others = held(lax.all_to_all(own, 'sp', 0, 0, tiled=True))  7.31 us
    all_to_all x1, blocking collectives, body(): powers = held(lax.all_to_all(power, 'tp', 0, 0, tiled=True))  6.36 us
    pallas_call x1, Pallas kernels, body(): pl.pallas_call(functools.partial(states_kernel, scale, root), grid=(width...  6.1 us
    pallas_call x1, Pallas kernels, body(): pl.pallas_call(functools.partial(totals_kernel, scale, root), grid=(width...  4.53 us
    pallas_call x1, Pallas kernels, body(): pl.pallas_call(functools.partial(norm_kernel, float(channels)), grid=(row...  3.81 us
  transfers between devices with their start and end apart: 1, of which 1 were waited for; matrix products, arithmetic and copies ran while one was open for 0% of the time, Pallas kernels for 0%

profile of v3, /device:TPU:0, one launch (start us, length us, event | category | flops | bytes accessed | tf_op | source)
XLA Modules:
  0.0 35.5 jit_solution(7109473202315660152)
XLA Ops:
  0.0 4.5 %totals.1 = (f32[8,4,1024]{2,1,0:T(4,128)}, f32[8,1024]{1,0:T(8,128)S(1)}, f32[8,1024]{1,0:T(8,128)S(1)}, f32[8,1024]{1,0:T(8,128)S(1)}) custom-call(f32[512,1024]{1,0:T(8,128)} %bitcast.6, bf16[512,1024]{1,0:T(8,128)(2,1)} %bitcast.8), custom_call_target="tpu_custom_call" | custom-call | tf_op jit(solution)/shard_map/totals/pallas_call | solution.py:176
  4.5 7.3 %all-to-all-start = ((f32[8,4,1024]{2,1,0:T(4,128)}), f32[8,4,1024]{2,1,0:T(4,128)S(1)}, u32[]{:S(2)}, u32[]{:S(2)}) async-start(f32[8,4,1024]{2,1,0:T(4,128)} %get-tuple-element.11), calls=%async_computation | async-start | bytes 262144 | tf_op jit(solution)/shard_map/all_to_all | solution.py:185
  11.8 7.3 %all-to-all-done.all_ref = f32[8,4,1024]{2,1,0:T(4,128)S(1)} async-done(((f32[8,4,1024]{2,1,0:T(4,128)}), f32[8,4,1024]{2,1,0:T(4,128)S(1)}, u32[]{:S(2)}, u32[]{:S(2)}) %all-to-all-start) | async-done | bytes 131104 | tf_op jit(solution)/shard_map/all_to_all | solution.py:185
  19.2 6.1 %states.1 = (f32[512,1024]{1,0:T(8,128)}, f32[4,4,128]{2,1,0:T(4,128)S(1)}) custom-call(s32[1]{0:T(128)} %bitcast.mine_ref, f32[8,4,1024]{2,1,0:T(4,128)S(1)} %all-to-all-done.all_ref, f32[8,1024]{1,0:T(8,128)S(1)} %get-tuple-element.12.prod_ref, f32[8,1024]{1,0:T(8,128)S(1)} %get-tuple-element.13.first_ref, f32[8,1024]{1,0:T(8,128)S(1)} %get-tuple-element.14.last_ref, ...), custom_call_target="tpu_custom_call" | custom-call | tf_op jit(solution)/shard_map/states/pallas_call | solution.py:187
  25.3 6.4 %all_to_all.10.power_ref = f32[4,4,128]{2,1,0:T(4,128)S(1)} all-to-all(f32[4,4,128]{2,1,0:T(4,128)S(1)} %get-tuple-element.15), channel_id=1, replica_groups=mesh['sp'=8,'tp'=4] {'tp'}, dimensions={0} | all-to-all | bytes 16384 | tf_op jit(solution)/shard_map/all_to_all | solution.py:207
  31.6 3.8 %norm.1 = bf16[512,1024]{1,0:T(8,128)(2,1)} custom-call(f32[4,4,128]{2,1,0:T(4,128)S(1)} %all_to_all.10.power_ref, f32[1,1024]{1,0:T(1,128)} %bitcast.11, f32[512,1024]{1,0:T(8,128)} %get-tuple-element.16.gated_ref), custom_call_target="tpu_custom_call" | custom-call | tf_op jit(solution)/shard_map/norm/pallas_call | solution.py:209
Async XLA Ops:
  4.5 14.7 %all-to-all-start = ((f32[8,4,1024]{2,1,0:T(4,128)}), f32[8,4,1024]{2,1,0:T(4,128)S(1)}, u32[]{:S(2)}, u32[]{:S(2)}) async-start(f32[8,4,1024]{2,1,0:T(4,128)} %get-tuple-element.11), calls=%async_computation | async-start | bytes 262144 | tf_op jit(solution)/shard_map/all_to_all | solution.py:185
